TPU v7x, 256 devices: a whole 4x4x8 slice. The times are simulated.
256 devices in a mesh: dp: 64 (over z, x, core), outer: 4 (over y).
Axes of the slice: x: 4, y: 4, z: 8, core: 2. Of those that a mesh axis runs over, the one named last changes fastest.
Arguments:
- partials: bfloat16 [4, 64, 2, 128, 8192], P('outer', 'dp'), may hold values from -3500 to 3500, as said below
- master: float32 [2, 128, 8192], P(None, 'dp'), may hold values from -6 to 6
- m_codes: bfloat16 [2, 128, 8192], P(None, 'dp'), may hold values from -1 to 1
- v_codes: bfloat16 [2, 128, 8192], P(None, 'dp'), may hold values from 0.049804688 to 1
- m_scales: float32 [2, 128, 4], P(None, 'dp'), may hold values from 0.0001 to 0.001
- v_scales: float32 [2, 128, 4], P(None, 'dp'), may hold values from 1e-08 to 1e-07
Outputs:
- new_master: float32 [2, 128, 8192], P(None, 'dp')
- new_m_codes: bfloat16 [2, 128, 8192], P(None, 'dp')
- new_v_codes: bfloat16 [2, 128, 8192], P(None, 'dp')
- new_m_scales: float32 [2, 128, 4], P(None, 'dp')
- new_v_scales: float32 [2, 128, 4], P(None, 'dp')
- weights: bfloat16 [2, 128, 8192], replicated
Inputs may be any that keep to these rules, and one draw needn't show every extreme that they name: Gradient partials of real values; entries vary from row to row and column to column.
All inputs are finite; a program needn't handle non-finite values. Where the computation divides by a largest or mean magnitude, that divisor is 1e-20 or more.
Results may differ from a plain program's by a relative error of at most 0.0004.
Values may be sent and summed in bfloat16 or wider, within the bound.
A program may use at most 64 MiB of HBM per device.

v0:
```python
import functools
import jax
import jax.numpy as jnp
from jax import lax
from jax.sharding import Mesh
from jax.sharding import PartitionSpec as P

BLOCK = 2048
STEP = 10
DP = ("dp_0", "dp_1", "dp_2")
DP_OUTER = ("dp_0", "dp_1", "dp_2", "outer")


def cut_along(x, dim, count):
    lengths = x.shape
    pieces = x.reshape(*lengths[:dim], count, lengths[dim] // count, *lengths[dim + 1 :])
    return jnp.moveaxis(pieces, dim, 0)


def sum_at_owner(x, axis, dim):
    pieces = cut_along(x, dim, lax.axis_size(axis))
    arrived = lax.all_to_all(pieces, axis, split_axis=0, concat_axis=0, tiled=True)
    return arrived.sum(axis=0)


def over_axes(x, axes):
    return functools.reduce(lax.psum, axes, x)


def sent_together(arrays, axis, dim, along):
    widths = [a.shape[along] for a in arrays]
    both = jnp.concatenate(arrays, axis=along)
    result = lax.all_gather(both, axis, axis=dim, tiled=True)
    return tuple(jnp.split(result, [sum(widths[:k]) for k in range(1, len(widths))], axis=along))


def in_order(pieces, dim):
    lengths = list(pieces.shape[1:])
    lengths[dim] *= pieces.shape[0]
    return jnp.moveaxis(pieces, 0, dim).reshape(lengths)


def gather_in_order(x, axes, order):
    pieces = x[None]
    for k in order:
        pieces = lax.all_gather(pieces, axes[k], axis=0, tiled=True)
    block = [lax.axis_size(axes[k]) for k in reversed(order)]
    pieces = pieces.reshape(*block, *x.shape)
    turned = sorted(range(len(order)), key=lambda place: order[len(order) - 1 - place])
    return pieces.transpose(*turned, *range(len(order), pieces.ndim)).reshape(-1, *x.shape)


def whole_of(x, axes, order, dim):
    return in_order(gather_in_order(x, axes, order), dim)


def adam_blocks(gradient, master, m_codes, v_codes, m_scales, v_scales, clip_factor):
    count = gradient.shape[0]
    rows = gradient.shape[1]
    blocks = gradient.shape[2] // BLOCK
    shape_four = (count, rows, blocks, BLOCK)
    moment = m_codes.astype(jnp.float32).reshape(shape_four) * m_scales[..., None]
    second = v_codes.astype(jnp.float32).reshape(shape_four) * v_scales[..., None]
    scaled = clip_factor * gradient.reshape(shape_four)
    moment = 0.9 * moment + 0.1 * scaled
    second = 0.95 * second + 0.05 * scaled * scaled
    update = moment / (1.0 - 0.9**STEP) / (jnp.sqrt(second / (1.0 - 0.95**STEP)) + 1e-08)
    fresh = master - 0.01 * update.reshape(master.shape)
    m_top = jnp.max(jnp.abs(moment), axis=3) + 1e-20
    v_top = jnp.max(jnp.abs(second), axis=3) + 1e-20
    m_next = (moment / m_top[..., None]).astype(jnp.bfloat16).reshape(master.shape)
    v_next = (second / v_top[..., None]).astype(jnp.bfloat16).reshape(master.shape)
    return (fresh, m_next, v_next, m_top, v_top, fresh.astype(jnp.bfloat16))


def body(partials, master, m_codes, v_codes, m_scales, v_scales):
    own_terms = partials[0, 0]
    received = lax.all_to_all(own_terms[None], "outer", split_axis=3, concat_axis=0, tiled=True)
    column_part = jnp.sum(received.astype(jnp.float32), axis=0)
    gradient = sum_at_owner(column_part, DP, 1)
    total = over_axes(jnp.sum(gradient * gradient), DP_OUTER)
    clip_factor = 1.0 / jnp.maximum(jnp.sqrt(total), 1.0)
    quarter = gradient.shape[2]
    offset = lax.axis_index("outer") * quarter
    scale_count = quarter // BLOCK
    scale_offset = lax.axis_index("outer") * scale_count
    results = adam_blocks(
        gradient,
        lax.dynamic_slice_in_dim(master, offset, quarter, 2),
        lax.dynamic_slice_in_dim(m_codes, offset, quarter, 2),
        lax.dynamic_slice_in_dim(v_codes, offset, quarter, 2),
        lax.dynamic_slice_in_dim(m_scales, scale_offset, scale_count, 2),
        lax.dynamic_slice_in_dim(v_scales, scale_offset, scale_count, 2),
        clip_factor,
    )
    fresh, m_next, v_next, m_top, v_top, rounded = results
    fresh, m_top, v_top = (
        lax.all_gather(fresh, "outer", axis=2, tiled=True),
        *sent_together((m_top, v_top), "outer", 2, 0),
    )
    m_next, v_next, rounded = sent_together((m_next, v_next, rounded), "outer", 2, 0)
    weights = whole_of(rounded, DP, (1, 0, 2), 1)
    return (fresh, m_next, v_next, m_top, v_top, weights)


def solution(mesh):
    finer = Mesh(
        mesh.devices.reshape(8, 4, 2, mesh.shape["outer"]), ("dp_0", "dp_1", "dp_2", "outer")
    )
    placed = (
        P("outer", DP, None, None, None),
        P(None, DP, None),
        P(None, DP, None),
        P(None, DP, None),
        P(None, DP, None),
        P(None, DP, None),
    )
    return jax.shard_map(
        body,
        mesh=finer,
        in_specs=placed,
        out_specs=(
            P(None, DP, None),
            P(None, DP, None),
            P(None, DP, None),
            P(None, DP, None),
            P(None, DP, None),
            P(),
        ),
        check_vma=False,
    )
```

profile of v0, /device:TPU:2, one launch (start us, length us, event | category | flops | bytes accessed | tf_op | source)
XLA Modules:
  0.0 303.8 jit_solution(3375123823743726198)
XLA Ops:
  7.2 11.2 %copy.36 = bf16[1,1,2,128,8192]{3,2,4,1,0:T(2,128)(2,1)} copy(bf16[1,1,2,128,8192]{4,3,2,1,0:T(8,128)(2,1)} %param.6) | data formatting | bytes 8388608 | tf_op args[0]
  18.3 53.3 %all_to_all.14 = bf16[1,2,128,8192]{2,1,0,3:T(2,128)(2,1)S(1)} all-to-all(bf16[1,2,128,8192]{2,1,0,3:T(2,128)(2,1)} %bitcast.21), channel_id=1, replica_groups=mesh['dp_0'=8,'dp_1'=4,'dp_2'=2,'outer'=4] {'outer'}, dimensions={3} | all-to-all | bytes 8388608 | tf_op jit(solution)/shard_map/all_to_all | solution.py:78
  71.6 5.1 %convert_reduce_fusion = f32[2,128,2048]{1,0,2:T(2,128)S(1)} fusion(bf16[2,128,4,2048]{1,0,3,2:T(2,128)(2,1)S(1)} %bitcast.18), kind=kLoop, calls=%fused_computation | loop fusion | flops 3670016 | bytes 6291456 | tf_op jit(solution)/shard_map/reduce_sum | solution.py:79
  76.7 3.5 %copy.37 = f32[2,128,2048]{2,0,1:T(2,128)} copy(f32[2,128,2048]{1,0,2:T(2,128)S(1)} %convert_reduce_fusion) | data formatting | bytes 4194304 | tf_op jit(solution)/shard_map/reduce_sum | solution.py:79
  80.2 4.9 %copy.38 = f32[64,2,2,2048]{3,2,1,0:T(2,128)} copy(f32[64,2,2,2048]{3,1,2,0:T(2,128)} %bitcast.22) | data formatting | bytes 4194304 | tf_op jit(solution)/shard_map/transpose | solution.py:17
  85.1 12.0 %all-to-all-start.1 = ((f32[64,2,2,2048]{3,2,1,0:T(2,128)}), f32[64,2,2,2048]{3,2,1,0:T(2,128)S(1)}, u32[]{:S(2)}, u32[]{:S(2)}) async-start(f32[64,2,2,2048]{3,2,1,0:T(2,128)} %copy.38), calls=%async_computation.1 | async-start | bytes 4194304 | tf_op jit(solution)/shard_map/all_to_all | solution.py:22
  97.1 0.0 all-gather.4.cloned.1.call-start
  97.2 0.2 dynamic-slice_reduce_fusion
  97.4 51.0 %all-to-all-done.1 = f32[64,2,2,2048]{3,2,1,0:T(2,128)S(1)} async-done(((f32[64,2,2,2048]{3,2,1,0:T(2,128)}), f32[64,2,2,2048]{3,2,1,0:T(2,128)S(1)}, u32[]{:S(2)}, u32[]{:S(2)}) %all-to-all-start.1) | async-done | bytes 2097184 | tf_op jit(solution)/shard_map/all_to_all | solution.py:22
  148.4 0.8 reduce_sum.28
  149.2 0.6 multiply_reduce_fusion
  149.8 15.4 %psum.28 = f32[]{:T(128)} all-reduce(f32[]{:T(128)} %multiply_reduce_fusion), channel_id=1, replica_groups=mesh['dp_0'=8,'dp_1'=4,'dp_2'=2,'outer'=4] {'dp_0'}, use_global_device_ids=true, to_apply=%region_3.0 | all-reduce | flops 1 | bytes 8 | tf_op jit(solution)/shard_map/psum | solution.py:27
  165.2 9.2 %psum.29 = f32[]{:T(128)} all-reduce(f32[]{:T(128)} %psum.28), channel_id=1, replica_groups=mesh['dp_0'=8,'dp_1'=4,'dp_2'=2,'outer'=4] {'dp_1'}, use_global_device_ids=true, to_apply=%region_4.0 | all-reduce | flops 1 | bytes 8 | tf_op jit(solution)/shard_map/psum | solution.py:27
  174.4 3.1 %psum.30 = f32[]{:T(128)} all-reduce(f32[]{:T(128)} %psum.29), channel_id=1, replica_groups=mesh['dp_0'=8,'dp_1'=4,'dp_2'=2,'outer'=4] {'dp_2'}, use_global_device_ids=true, to_apply=%region_5.0 | all-reduce | flops 1 | bytes 8 | tf_op jit(solution)/shard_map/psum | solution.py:27
  177.5 9.5 %psum.31 = f32[]{:T(128)} all-reduce(f32[]{:T(128)} %psum.30), channel_id=1, replica_groups=mesh['dp_0'=8,'dp_1'=4,'dp_2'=2,'outer'=4] {'outer'}, use_global_device_ids=true, to_apply=%region_6.0 | all-reduce | flops 1 | bytes 8 | tf_op jit(solution)/shard_map/psum | solution.py:27
  187.7 1.0 abs_reduce_fusion.1
  188.7 0.9 fusion.4
  189.6 0.1 pad_maximum_fusion
  189.6 12.1 %all_gather.19 = bf16[6,2,8192]{2,1,0:T(2,128)(2,1)S(1)} all-gather(bf16[6,2,2048]{2,1,0:T(2,128)(2,1)S(1)} %pad_maximum_fusion), channel_id=1, replica_groups=mesh['dp_0'=8,'dp_1'=4,'dp_2'=2,'outer'=4] {'outer'}, dimensions={2}, use_global_device_ids=true | all-gather | bytes 245760 | tf_op jit(solution)/shard_map/all_gather | solution.py:33
  201.8 0.8 fusion.5
  202.6 12.4 %all-gather = bf16[8,2,8192]{2,1,0:T(2,128)(2,1)} all-gather(bf16[2,2,8192]{2,1,0:T(2,128)(2,1)S(1)} %get-tuple-element.48), channel_id=2, replica_groups=mesh['dp_0'=8,'dp_1'=4,'dp_2'=2,'outer'=4] {'dp_1'}, dimensions={0}, use_global_device_ids=true | all-gather | bytes 327680 | tf_op jit(solution)/shard_map/all_gather | solution.py:46
  215.0 38.6 %all-gather.4.cloned.1.call-done = bf16[32,2,2,8192]{3,2,1,0:T(2,128)(2,1)} async-done(((bf16[4,2,2,8192]{3,2,1,0:T(2,128)(2,1)}), bf16[32,2,2,8192]{3,2,1,0:T(2,128)(2,1)}) %all-gather.4.cloned.1.call-update) | async-done | bytes 2097168 | tf_op jit(solution)/shard_map/all_gather | solution.py:46
  253.6 0.1 copy.39
  253.7 9.7 %all_gather.20 = f32[4,2,4]{0,1,2:T(2,128)S(1)} all-gather(f32[4,2,1]{0,1,2:T(2,128)S(1)} %copy.39), channel_id=1, replica_groups=mesh['dp_0'=8,'dp_1'=4,'dp_2'=2,'outer'=4] {'outer'}, dimensions={2}, use_global_device_ids=true | all-gather | bytes 160 | tf_op jit(solution)/shard_map/all_gather | solution.py:33
  263.4 12.2 %all_gather.18 = f32[2,2,8192]{2,1,0:T(2,128)S(1)} all-gather(f32[2,2,2048]{2,1,0:T(2,128)S(1)} %get-tuple-element.47), channel_id=1, replica_groups=mesh['dp_0'=8,'dp_1'=4,'dp_2'=2,'outer'=4] {'outer'}, dimensions={2}, use_global_device_ids=true | all-gather | bytes 163840 | tf_op jit(solution)/shard_map/all_gather | solution.py:98
  275.6 0.1 fusion.6
  275.6 0.7 copy.42
  276.3 0.7 copy.43
  277.0 6.1 %copy.40 = bf16[2,8,4,2,2,8192]{5,4,3,0,2,1:T(2,128)(2,1)S(1)} copy(bf16[2,8,4,2,2,8192]{5,4,3,2,1,0:T(2,128)(2,1)} %bitcast.23) | data formatting | bytes 8388608 | tf_op jit(solution)/shard_map/reshape | solution.py:48
  283.1 6.3 %copy.41 = bf16[2,64,2,8192]{3,0,2,1:T(2,128)(2,1)} copy(bf16[2,64,2,8192]{3,2,0,1:T(2,128)(2,1)S(1)} %bitcast.19) | data formatting | bytes 8388608 | tf_op jit(solution)/shard_map/transpose | solution.py:40
  289.4 6.9 %copy.44 = bf16[2,128,8192]{2,1,0:T(8,128)(2,1)} copy(bf16[2,128,8192]{2,0,1:T(2,128)(2,1)} %bitcast.20) | data formatting | bytes 8388608
  296.3 0.7 copy.46
  (11 shorter events, 0.1 us)
Async XLA Ops:
  80.2 17.0 %copy-start = (f32[2,2,4]{2,1,0:T(2,128)S(1)}, f32[2,2,4]{2,1,0:T(2,128)}, u32[]{:S(2)}) copy-start(f32[2,2,4]{2,1,0:T(2,128)} %param.11) | copy-start | bytes 196
  80.2 17.0 %copy-start.1 = (f32[2,2,4]{2,1,0:T(2,128)S(1)}, f32[2,2,4]{2,1,0:T(2,128)}, u32[]{:S(2)}) copy-start(f32[2,2,4]{2,1,0:T(2,128)} %param.10) | copy-start | bytes 196
  85.1 63.3 %all-to-all-start.1 = ((f32[64,2,2,2048]{3,2,1,0:T(2,128)}), f32[64,2,2,2048]{3,2,1,0:T(2,128)S(1)}, u32[]{:S(2)}, u32[]{:S(2)}) async-start(f32[64,2,2,2048]{3,2,1,0:T(2,128)} %copy.38), calls=%async_computation.1 | async-start | bytes 4194304 | tf_op jit(solution)/shard_map/all_to_all | solution.py:22
  97.1 156.4 %all-gather.4.cloned.1.call-start = ((), (), s32[]{:S(2)}) async-start(), calls=%async_computation.2 | async-start | bytes 2359296 | tf_op jit(solution)/shard_map/all_gather | solution.py:46
  214.9 62.0 %all-gather.6.cloned.1.call-start = ((), (), s32[]{:S(2)}) async-start(), calls=%async_computation.3 | async-start | bytes 6291456 | tf_op jit(solution)/shard_map/all_gather | solution.py:46
Sparse Core Ops, SparseCore 0:
  215.1 38.4 all-gather.3
  255.3 17.5 all-gather.5
where the time goes:
time: 305 us; the launch traced here: 304 us
  blocking collectives  137 us (45%)
  waiting for transfers between devices  89.6 us (29%)
  local copies, waits for them, and re-layouts  42 us (14%)
  between operations  14.8 us (5%)
  starting transfers between devices  12.1 us (4%)
  other arithmetic  8.43 us (3%)
    all_to_all x1, blocking collectives, body(): lax.all_to_all(own_terms[None], 'outer', split_axis=3, concat_axis=0, til...  53.3 us
    all_to_all x1, waiting for transfers between devices, sum_at_owner(): lax.all_to_all(pieces, axis, split_axis=0, concat_axis=0, tiled=True)  51 us
    all_gather x2, waiting for transfers between devices, gather_in_order(): pieces = lax.all_gather(pieces, axes[k], axis=0, tiled=True)  38.6 us
    psum x4, blocking collectives, over_axes(): return functools.reduce(lax.psum, axes, x)  37.2 us
    all_gather x2, blocking collectives, sent_together(): result = lax.all_gather(both, axis, axis=dim, tiled=True)  21.8 us
    unnamed x9, local copies, waits for them, and re-layouts  20 us
    all_gather x1, blocking collectives, gather_in_order(): pieces = lax.all_gather(pieces, axes[k], axis=0, tiled=True)  12.4 us
    all_gather x1, blocking collectives, body(): lax.all_gather(fresh, 'outer', axis=2, tiled=True)  12.2 us
  transfers between devices with their start and end apart: 3, of which 2 were waited for; matrix products, arithmetic and copies ran while one was open for 1% of the time, Pallas kernels for 0%

commit v1 on v0

--- a/solution.py
+++ b/solution.py
@@ -75,7 +75,16 @@
 
 def body(partials, master, m_codes, v_codes, m_scales, v_scales):
     own_terms = partials[0, 0]
-    received = lax.all_to_all(own_terms[None], "outer", split_axis=3, concat_axis=0, tiled=True)
+    in_array = own_terms[None]
+    received = jnp.concatenate(
+        lax.all_to_all(
+            jnp.stack(jnp.split(in_array, lax.axis_size("outer"), 3)),
+            "outer",
+            split_axis=0,
+            concat_axis=0,
+        ),
+        0,
+    )
     column_part = jnp.sum(received.astype(jnp.float32), axis=0)
     gradient = sum_at_owner(column_part, DP, 1)
     total = over_axes(jnp.sum(gradient * gradient), DP_OUTER)

time: 305 us -> 288 us (0.944)
  local copies, waits for them, and re-layouts: 42 us -> 30 us
  other arithmetic: 8.43 us -> 4.71 us
    unnamed x9 -> x8, local copies, waits for them, and re-layouts: 20 us -> 8.89 us
    reduce_sum x1, other arithmetic: 5.08 us -> 0.79 us  [body(): column_part = jnp.sum(received.astype(jnp.float32), axis=0)]
where the time goes in v1:
time: 288 us
  blocking collectives  137 us (48%)
  waiting for transfers between devices  89.6 us (31%)
  local copies, waits for them, and re-layouts  30 us (10%)
  between operations  14.9 us (5%)
  starting transfers between devices  12.1 us (4%)
  other arithmetic  4.71 us (2%)
    all_to_all x1, blocking collectives, body(): lax.all_to_all(jnp.stack(jnp.split(in_array, lax.axis_size('outer'), 3)),...  53.1 us
    all_to_all x1, waiting for transfers between devices, sum_at_owner(): lax.all_to_all(pieces, axis, split_axis=0, concat_axis=0, tiled=True)  51 us
    all_gather x2, waiting for transfers between devices, gather_in_order(): pieces = lax.all_gather(pieces, axes[k], axis=0, tiled=True)  38.6 us
    psum x4, blocking collectives, over_axes(): return functools.reduce(lax.psum, axes, x)  37.2 us
    all_gather x2, blocking collectives, sent_together(): result = lax.all_gather(both, axis, axis=dim, tiled=True)  21.8 us
    all_gather x1, blocking collectives, gather_in_order(): pieces = lax.all_gather(pieces, axes[k], axis=0, tiled=True)  12.4 us
    all_gather x1, blocking collectives, body(): lax.all_gather(fresh, 'outer', axis=2, tiled=True)  12.2 us
    all_to_all x1, starting transfers between devices, sum_at_owner(): lax.all_to_all(pieces, axis, split_axis=0, concat_axis=0, tiled=True)  12 us
  transfers between devices with their start and end apart: 3, of which 2 were waited for; matrix products, arithmetic and copies ran while one was open for 1% of the time, Pallas kernels for 0%

profile of v1, /device:TPU:2, one launch (start us, length us, event | category | flops | bytes accessed | tf_op | source)
XLA Modules:
  0.0 287.9 jit_solution(633560168804519845)
XLA Ops:
  7.2 2.8 slice_bitcast_fusion.3
  9.9 0.6 pad_maximum_fusion
  10.5 53.1 %all_to_all.10 = bf16[4,1,2,128,2048]{4,3,2,1,0:T(8,128)(2,1)S(1)} all-to-all(bf16[4,1,2,128,2048]{4,3,2,1,0:T(8,128)(2,1)S(1)} %pad_maximum_fusion), channel_id=1, replica_groups=mesh['dp_0'=8,'dp_1'=4,'dp_2'=2,'outer'=4] {'outer'}, dimensions={0} | all-to-all | bytes 8388608 | tf_op jit(solution)/shard_map/all_to_all | solution.py:80
  63.6 0.8 convert_reduce_fusion
  64.4 1.6 copy.33
  66.0 3.2 %copy.34 = f32[64,2,2,2048]{3,2,1,0:T(2,128)} copy(f32[64,2,2,2048]{3,1,2,0:T(2,128)S(1)} %bitcast.26) | data formatting | bytes 4194304 | tf_op jit(solution)/shard_map/transpose | solution.py:17
  69.2 12.0 %all-to-all-start.1 = ((f32[64,2,2,2048]{3,2,1,0:T(2,128)}), f32[64,2,2,2048]{3,2,1,0:T(2,128)S(1)}, u32[]{:S(2)}, u32[]{:S(2)}) async-start(f32[64,2,2,2048]{3,2,1,0:T(2,128)} %copy.34), calls=%async_computation.1 | async-start | bytes 4194304 | tf_op jit(solution)/shard_map/all_to_all | solution.py:22
  81.3 0.2 dynamic-slice_reduce_fusion
  81.5 51.0 %all-to-all-done.1 = f32[64,2,2,2048]{3,2,1,0:T(2,128)S(1)} async-done(((f32[64,2,2,2048]{3,2,1,0:T(2,128)}), f32[64,2,2,2048]{3,2,1,0:T(2,128)S(1)}, u32[]{:S(2)}, u32[]{:S(2)}) %all-to-all-start.1) | async-done | bytes 2097184 | tf_op jit(solution)/shard_map/all_to_all | solution.py:22
  132.5 0.8 reduce_sum.28
  133.3 0.6 multiply_reduce_fusion
  133.9 15.4 %psum.28 = f32[]{:T(128)} all-reduce(f32[]{:T(128)} %multiply_reduce_fusion), channel_id=1, replica_groups=mesh['dp_0'=8,'dp_1'=4,'dp_2'=2,'outer'=4] {'dp_0'}, use_global_device_ids=true, to_apply=%region_3.0 | all-reduce | flops 1 | bytes 8 | tf_op jit(solution)/shard_map/psum | solution.py:27
  149.3 9.2 %psum.29 = f32[]{:T(128)} all-reduce(f32[]{:T(128)} %psum.28), channel_id=1, replica_groups=mesh['dp_0'=8,'dp_1'=4,'dp_2'=2,'outer'=4] {'dp_1'}, use_global_device_ids=true, to_apply=%region_4.0 | all-reduce | flops 1 | bytes 8 | tf_op jit(solution)/shard_map/psum | solution.py:27
  158.5 3.1 %psum.30 = f32[]{:T(128)} all-reduce(f32[]{:T(128)} %psum.29), channel_id=1, replica_groups=mesh['dp_0'=8,'dp_1'=4,'dp_2'=2,'outer'=4] {'dp_2'}, use_global_device_ids=true, to_apply=%region_5.0 | all-reduce | flops 1 | bytes 8 | tf_op jit(solution)/shard_map/psum | solution.py:27
  161.6 9.5 %psum.31 = f32[]{:T(128)} all-reduce(f32[]{:T(128)} %psum.30), channel_id=1, replica_groups=mesh['dp_0'=8,'dp_1'=4,'dp_2'=2,'outer'=4] {'outer'}, use_global_device_ids=true, to_apply=%region_6.0 | all-reduce | flops 1 | bytes 8 | tf_op jit(solution)/shard_map/psum | solution.py:27
  171.9 1.0 abs_reduce_fusion.1
  172.8 0.9 fusion.4
  173.7 0.1 pad_maximum_fusion.1
  173.8 12.1 %all_gather.19 = bf16[6,2,8192]{2,1,0:T(2,128)(2,1)S(1)} all-gather(bf16[6,2,2048]{2,1,0:T(2,128)(2,1)S(1)} %pad_maximum_fusion.1), channel_id=1, replica_groups=mesh['dp_0'=8,'dp_1'=4,'dp_2'=2,'outer'=4] {'outer'}, dimensions={2}, use_global_device_ids=true | all-gather | bytes 245760 | tf_op jit(solution)/shard_map/all_gather | solution.py:33
  185.9 0.8 fusion.5
  186.7 12.4 %all-gather = bf16[8,2,8192]{2,1,0:T(2,128)(2,1)} all-gather(bf16[2,2,8192]{2,1,0:T(2,128)(2,1)S(1)} %get-tuple-element.52), channel_id=2, replica_groups=mesh['dp_0'=8,'dp_1'=4,'dp_2'=2,'outer'=4] {'dp_1'}, dimensions={0}, use_global_device_ids=true | all-gather | bytes 327680 | tf_op jit(solution)/shard_map/all_gather | solution.py:46
  199.1 38.6 %all-gather.4.cloned.1.call-done = bf16[32,2,2,8192]{3,2,1,0:T(2,128)(2,1)} async-done(((bf16[4,2,2,8192]{3,2,1,0:T(2,128)(2,1)}), bf16[32,2,2,8192]{3,2,1,0:T(2,128)(2,1)}) %all-gather.4.cloned.1.call-update) | async-done | bytes 2097168 | tf_op jit(solution)/shard_map/all_gather | solution.py:46
  237.7 0.1 copy.35
  237.8 9.7 %all_gather.20 = f32[4,2,4]{0,1,2:T(2,128)S(1)} all-gather(f32[4,2,1]{0,1,2:T(2,128)S(1)} %copy.35), channel_id=1, replica_groups=mesh['dp_0'=8,'dp_1'=4,'dp_2'=2,'outer'=4] {'outer'}, dimensions={2}, use_global_device_ids=true | all-gather | bytes 160 | tf_op jit(solution)/shard_map/all_gather | solution.py:33
  247.5 0.1 fusion.6
  247.6 0.7 copy.38
  248.3 0.7 copy.39
  248.9 12.2 %all_gather.18 = f32[2,2,8192]{2,1,0:T(2,128)S(1)} all-gather(f32[2,2,2048]{2,1,0:T(2,128)S(1)} %get-tuple-element.47), channel_id=1, replica_groups=mesh['dp_0'=8,'dp_1'=4,'dp_2'=2,'outer'=4] {'outer'}, dimensions={2}, use_global_device_ids=true | all-gather | bytes 163840 | tf_op jit(solution)/shard_map/all_gather | solution.py:107
  261.1 6.1 %copy.36 = bf16[2,8,4,2,2,8192]{5,4,3,0,2,1:T(2,128)(2,1)S(1)} copy(bf16[2,8,4,2,2,8192]{5,4,3,2,1,0:T(2,128)(2,1)} %bitcast.28) | data formatting | bytes 8388608 | tf_op jit(solution)/shard_map/reshape | solution.py:48
  267.2 6.3 %copy.37 = bf16[2,64,2,8192]{3,0,2,1:T(2,128)(2,1)} copy(bf16[2,64,2,8192]{3,2,0,1:T(2,128)(2,1)S(1)} %bitcast.24) | data formatting | bytes 8388608 | tf_op jit(solution)/shard_map/transpose | solution.py:40
  273.5 6.9 %copy.40 = bf16[2,128,8192]{2,1,0:T(8,128)(2,1)} copy(bf16[2,128,8192]{2,0,1:T(2,128)(2,1)} %bitcast.25) | data formatting | bytes 8388608
  280.4 0.7 copy.42
  (12 shorter events, 0.1 us)
Async XLA Ops:
  66.0 15.3 %copy-start = (f32[2,2,4]{2,1,0:T(2,128)S(1)}, f32[2,2,4]{2,1,0:T(2,128)}, u32[]{:S(2)}) copy-start(f32[2,2,4]{2,1,0:T(2,128)} %param.11) | copy-start | bytes 196
  66.0 15.3 %copy-start.1 = (f32[2,2,4]{2,1,0:T(2,128)S(1)}, f32[2,2,4]{2,1,0:T(2,128)}, u32[]{:S(2)}) copy-start(f32[2,2,4]{2,1,0:T(2,128)} %param.10) | copy-start | bytes 196
  69.2 63.3 %all-to-all-start.1 = ((f32[64,2,2,2048]{3,2,1,0:T(2,128)}), f32[64,2,2,2048]{3,2,1,0:T(2,128)S(1)}, u32[]{:S(2)}, u32[]{:S(2)}) async-start(f32[64,2,2,2048]{3,2,1,0:T(2,128)} %copy.34), calls=%async_computation.1 | async-start | bytes 4194304 | tf_op jit(solution)/shard_map/all_to_all | solution.py:22
  81.3 156.4 %all-gather.4.cloned.1.call-start = ((), (), s32[]{:S(2)}) async-start(), calls=%async_computation.2 | async-start | bytes 2359296 | tf_op jit(solution)/shard_map/all_gather | solution.py:46
  199.1 62.0 %all-gather.6.cloned.1.call-start = ((), (), s32[]{:S(2)}) async-start(), calls=%async_computation.3 | async-start | bytes 6291456 | tf_op jit(solution)/shard_map/all_gather | solution.py:46
Sparse Core Ops, SparseCore 0:
  199.2 38.4 all-gather.3
  239.5 17.5 all-gather.5
